TPU v7x, 256 devices: a whole 4x4x8 slice. The times are simulated.
256 devices in a mesh: lat: 16 (over y, x_lo, core), lon: 16 (over z, x_hi).
Axes of the slice: x: 4 (x_hi: 2, x_lo: 2; x = x_hi * 2 + x_lo), y: 4, z: 8, core: 2. Of those that a mesh axis runs over, the one named last changes fastest.
Arguments:
- adjoint: float32 [8, 8, 512, 2048], P(None, None, 'lat', 'lon'), may hold values from -6 to 6
- transport: float32 [6, 8, 512, 2048], P(None, None, 'lat', 'lon'), may hold values from 0.03 to 0.14
- cell_weight: float32 [512, 2048], P('lat', 'lon'), may hold values from 0.1 to 1
- region_local: int32 [512, 2048], P('lat', 'lon'), may hold values from 0 to 255
- tile_regions: int32 [256, 256], replicated, may hold values from 0 to 16383, as said below
- polar_rows: int32 [512], P('lat'), may hold values 0 or 1
- week_index: int32 [1], replicated, may hold values from 0 to 51
- grad_in: bfloat16 [16384, 416], P(('lat', 'lon')), may hold values from -6 to 6
- covariance: bfloat16 [16384, 16384], P(('lat', 'lon')), may hold values from -0.1875 to 0.1875
Outputs:
- adjoint_out: float32 [8, 8, 512, 2048], P(None, None, 'lat', 'lon')
- precond: float32 [16384, 416], P(('lat', 'lon'))
Inputs may be any that keep to these rules, and one draw needn't show every extreme that they name: `tile_regions`: each row holds 256 different region numbers; with per = 1, entries o * per to o * per + per - 1 of a row lie in regions o * 64 to o * 64 + 63, for every o.
All inputs are finite; a program needn't handle non-finite values. No bound on the sum of `polar_rows` on one device may be relied on, other than what follows from the above.
Results may differ from a plain program's by a relative error of at most 0.00066.
Values may be sent and summed in bfloat16 or wider, within the bound.
A program may use at most 128 MiB of HBM per device.

v0:
```python
import functools
import jax
import jax.numpy as jnp
from jax import lax
from jax.sharding import Mesh
from jax.sharding import PartitionSpec as P

LON = ("lon_0", "lon_1")
LAT_LON = ("lat", "lon_0", "lon_1")


def extended_2(x, sides, width):
    for axis, dim in sides:
        size, length = (lax.axis_size(axis), x.shape[dim])
        up = [(i, (i + 1) % size) for i in range(size)]
        down = [(j, i) for i, j in up]
        last = lax.slice_in_dim(x, length - width, length, axis=dim)
        leading = lax.slice_in_dim(x, 0, width, axis=dim)
        before = lax.ppermute(last, axis, up)
        after = lax.ppermute(leading, axis, down)
        x = jnp.concatenate([before, x, after], axis=dim)
    return x


def one_axis_at_a_time(x, axes):
    return functools.reduce(lax.psum, axes, x)


def advance(padded, rates):
    centre = padded[:, :, 1:-1, 1:-1]
    to_east = padded[:, :, 1:-1, 2:] - centre
    to_west = padded[:, :, 1:-1, :-2] - centre
    to_north = padded[:, :, 2:, 1:-1] - centre
    to_south = padded[:, :, :-2, 1:-1] - centre
    flat_zero = jnp.zeros_like(centre[:, :1])
    upper = jnp.concatenate([centre[:, 1:] - centre[:, :-1], flat_zero], axis=1)
    lower = jnp.concatenate([flat_zero, centre[:, :-1] - centre[:, 1:]], axis=1)
    return (
        centre
        + rates[0] * to_east
        + rates[1] * to_west
        + rates[2] * to_north
        + rates[3] * to_south
        + rates[4] * upper
        + rates[5] * lower
    )


def pole_mask(padded, margin, interior):
    band = lax.axis_index("lat")
    last_band = lax.axis_size("lat") - 1
    row_ids = jnp.arange(interior + 2 * margin, dtype=jnp.int32)
    outside = (row_ids < margin) & (band == 0) | (row_ids >= interior + margin) & (
        band == last_band
    )
    return jnp.where(outside[None, None, :, None], 0.0, padded)


def shards(
    adjoint,
    transport,
    cell_weight,
    region_local,
    tile_regions,
    polar_rows,
    week_index,
    grad_in,
    covariance,
):
    tracers, levels, lat_rows, lon_cols = adjoint.shape
    region_count = covariance.shape[1]
    own_rows = covariance.shape[0]
    week_cols = grad_in.shape[1] // tracers
    lon_count = lax.axis_size(LON)
    my_tile = lax.axis_index("lat") * lon_count + lax.axis_index(LON)
    base = jnp.dot(
        covariance,
        lax.all_gather(grad_in, LAT_LON, axis=0, tiled=True),
        preferred_element_type=jnp.float32,
    )
    extended, rate_ext = (
        extended_2(adjoint, (("lat", 2), (LON, 3)), 2),
        extended_2(transport, (("lat", 2), (LON, 3)), 2),
    )
    extended = pole_mask(extended, 2, lat_rows)
    first = advance(extended, rate_ext[:, :, 1:-1, 1:-1])
    first = pole_mask(first, 1, lat_rows)
    field = advance(first, transport)
    row_sums = one_axis_at_a_time(jnp.sum(field, axis=3), LON)
    zonal = row_sums / (lon_cols * lon_count)
    flags = polar_rows.astype(jnp.float32)[None, None, :, None]
    adjoint_out = field + 0.5 * flags * (zonal[..., None] - field)
    surface = (adjoint_out[:, 0] * cell_weight[None]).reshape(tracers, -1)
    local_count = tile_regions.shape[1]
    one_hot = (
        region_local.reshape(1, -1) == jnp.arange(local_count, dtype=jnp.int32)[:, None]
    ).astype(jnp.float32)
    local_sums = lax.dot_general(
        one_hot,
        surface,
        (((1,), (1,)), ((), ())),
        precision=lax.Precision.HIGHEST,
        preferred_element_type=jnp.float32,
    )
    my_regions = lax.dynamic_index_in_dim(tile_regions, my_tile, 0, keepdims=False)
    dense = jnp.zeros((region_count, tracers), jnp.float32).at[my_regions].add(local_sums)
    fresh_all = lax.psum(dense, LAT_LON).astype(jnp.bfloat16)
    added = jnp.dot(covariance, fresh_all, preferred_element_type=jnp.float32)
    week_hot = (jnp.arange(week_cols, dtype=jnp.int32) == week_index[0]).astype(jnp.float32)
    precond = (
        base.reshape(own_rows, week_cols, tracers) + week_hot[None, :, None] * added[:, None, :]
    )
    return (adjoint_out, precond.reshape(own_rows, week_cols * tracers))


def solution(mesh):
    split = Mesh(mesh.devices.reshape(mesh.shape["lat"], 8, 2), ("lat", "lon_0", "lon_1"))
    placed = (
        P(None, None, "lat", LON),
        P(None, None, "lat", LON),
        P("lat", LON),
        P("lat", LON),
        P(),
        P("lat"),
        P(),
        P(LAT_LON, None),
        P(LAT_LON, None),
    )
    return jax.shard_map(
        shards,
        mesh=split,
        in_specs=placed,
        out_specs=(P(None, None, "lat", LON), P(LAT_LON, None)),
        check_vma=False,
    )
```

profile of v0, /device:TPU:96, one launch (start us, length us, event | category | flops | bytes accessed | tf_op | source)
XLA Modules:
  0.0 765.9 jit_solution(8474163198109357353)
XLA Ops:
  9.1 3.8 collective-permute-start.5
  15.3 3.9 collective-permute-start.1
  23.0 3.2 copy.74
  26.8 2.2 copy.73
  33.0 3.0 collective-permute-start.6
  37.4 2.6 copy.69
  49.0 4.4 maximum_bitcast_fusion.4
  53.4 3.5 copy.68
  56.9 3.4 copy.70
  63.8 2.3 collective-permute-start.3
  66.2 3.8 maximum_bitcast_fusion.3
  71.3 2.5 maximum_select_fusion
  73.8 4.2 slice_subtract_fusion.9
  78.1 6.4 fusion.4
  86.8 6.9 fusion.33
  93.7 28.0 %psum.21 = f32[8,8,32]{2,1,0:T(8,128)S(1)} all-reduce(f32[8,8,32]{2,1,0:T(8,128)S(1)} %get-tuple-element.10), channel_id=1, replica_groups=mesh['lat'=16,'lon_0'=8,'lon_1'=2] {'lon_0'}, use_global_device_ids=true, to_apply=%region_1.2 | all-reduce | flops 2048 | bytes 16384 | tf_op jit(solution)/shard_map/psum | solution.py:26
  121.7 12.6 %psum.22 = f32[8,8,32]{2,1,0:T(8,128)S(1)} all-reduce(f32[8,8,32]{2,1,0:T(8,128)S(1)} %psum.21), channel_id=1, replica_groups=mesh['lat'=16,'lon_0'=8,'lon_1'=2] {'lon_1'}, use_global_device_ids=true, to_apply=%region_2.3 | all-reduce | flops 2048 | bytes 16384 | tf_op jit(solution)/shard_map/psum | solution.py:26
  134.3 2.7 multiply_add_fusion
  138.9 3.8 copy.85
  145.0 5.2 scatter_custom_fusion
  150.2 144.0 %all-reduce.5 = bf16[16384,8]{1,0:T(8,128)(2,1)} all-reduce(f32[16384,8]{1,0:T(8,128)} %scatter_custom_fusion), channel_id=1, replica_groups=mesh['lat'=16,'lon_0'=8,'lon_1'=2] {'lat','lon_0','lon_1'}, use_global_device_ids=true, to_apply=%region_4.5 | all-reduce | flops 131072 | bytes 786432 | tf_op jit(solution)/shard_map/psum | solution.py:107
  294.2 3.4 fusion.27
  297.8 451.9 %all-gather.2.cloned.1.call-done = bf16[16384,416]{1,0:T(8,128)(2,1)} async-done(((bf16[64,416]{1,0:T(8,128)(2,1)}), bf16[16384,416]{1,0:T(8,128)(2,1)}) %all-gather.2.cloned.1.call-update) | async-done | bytes 13631504 | tf_op jit(solution)/shard_map/all_gather | solution.py:78
  749.6 9.4 %convolution_add_fusion = f32[64,416]{1,0:T(8,128)} fusion(bf16[64,16384]{1,0:T(8,128)(2,1)S(1)} %copy-done, bf16[16384,416]{1,0:T(8,128)(2,1)} %all-gather.2.cloned.1.call-done, f32[64,416]{1,0:T(8,128)S(1)} %copy.84, f32[416]{0:T(512)S(1)} %mul.213), kind=kOutput, calls=%fused_computation.43 | convolution fusion | flops 872468480 | bytes 15943296 | tf_op jit(solution)/shard_map/dot_general | solution.py:76
  (81 shorter events, 33.8 us)
Async XLA Ops:
  7.2 287.0 %copy-start = (bf16[64,16384]{1,0:T(8,128)(2,1)S(1)}, bf16[64,16384]{1,0:T(8,128)(2,1)}, u32[]{:S(2)}) copy-start(bf16[64,16384]{1,0:T(8,128)(2,1)} %param.17) | copy-start | bytes 6291460
  7.2 742.4 %all-gather.2.cloned.1.call-start = ((), (), s32[]{:S(2)}) async-start(), calls=%async_computation | async-start | bytes 16842752 | tf_op jit(solution)/shard_map/all_gather | solution.py:78
  9.0 17.8 %collective-permute-start.4 = (f32[6,8,2,128]{3,1,2,0:T(8,128)S(1)}, f32[6,8,2,128]{3,1,2,0:T(8,128)S(1)}, u32[]{:S(2)}, u32[]{:S(2)}) collective-permute-start(f32[6,8,2,128]{3,1,2,0:T(8,128)S(1)} %copy.89), channel_id=1, source_target_pairs={{0,16},{16,32},{32,48},{48,64},{64,80},{80,96},{96,112},{112,128},... | collective-permute-start | bytes 147464 | tf_op jit(solution)/shard_map/ppermute | solution.py:19
  9.1 19.9 %collective-permute-start.5 = (f32[6,8,2,128]{3,1,2,0:T(8,128)S(1)}, f32[6,8,2,128]{3,1,2,0:T(8,128)S(1)}, u32[]{:S(2)}, u32[]{:S(2)}) collective-permute-start(f32[6,8,2,128]{3,1,2,0:T(8,128)S(1)} %copy.90), channel_id=1, source_target_pairs={{16,0},{32,16},{48,32},{64,48},{80,64},{96,80},{112,96},{128,112},... | collective-permute-start | bytes 147464 | tf_op jit(solution)/shard_map/ppermute | solution.py:20
  14.7 38.8 %collective-permute-start = (f32[8,8,2,128]{3,1,2,0:T(8,128)}, f32[8,8,2,128]{3,1,2,0:T(8,128)}, u32[]{:S(2)}, u32[]{:S(2)}) collective-permute-start(f32[8,8,2,128]{3,1,2,0:T(8,128)} %copy.87), channel_id=1, source_target_pairs={{0,16},{16,32},{32,48},{48,64},{64,80},{80,96},{96,112},{112,128},... | collective-permute-start | bytes 196616 | tf_op jit(solution)/shard_map/ppermute | solution.py:19
  15.3 41.6 %collective-permute-start.1 = (f32[8,8,2,128]{3,1,2,0:T(8,128)}, f32[8,8,2,128]{3,1,2,0:T(8,128)}, u32[]{:S(2)}, u32[]{:S(2)}) collective-permute-start(f32[8,8,2,128]{3,1,2,0:T(8,128)} %copy.88), channel_id=1, source_target_pairs={{16,0},{32,16},{48,32},{64,48},{80,64},{96,80},{112,96},{128,112},... | collective-permute-start | bytes 196616 | tf_op jit(solution)/shard_map/ppermute | solution.py:20
  31.2 6.2 copy-start.14
  33.0 16.0 %collective-permute-start.6 = (f32[6,8,36,2]{2,1,3,0:T(8,128)}, f32[6,8,36,2]{2,1,3,0:T(8,128)}, u32[]{:S(2)}, u32[]{:S(2)}) collective-permute-start(f32[6,8,36,2]{2,1,3,0:T(8,128)} %get-tuple-element.20), channel_id=1, source_target_pairs={{0,1},{1,2},{2,3},{3,4},{4,5},{5,6},{6,7},{7,8},{8,9},{9,10},{10,1... | collective-permute-start | bytes 41480 | tf_op jit(solution)/shard_map/ppermute | solution.py:19
  36.0 13.0 %collective-permute-start.7 = (f32[6,8,36,2]{2,1,3,0:T(8,128)}, f32[6,8,36,2]{2,1,3,0:T(8,128)}, u32[]{:S(2)}, u32[]{:S(2)}) collective-permute-start(f32[6,8,36,2]{2,1,3,0:T(8,128)} %get-tuple-element.21), channel_id=1, source_target_pairs={{1,0},{2,1},{3,2},{4,3},{5,4},{6,5},{7,6},{8,7},{9,8},{10,9},{11,1... | collective-permute-start | bytes 41480 | tf_op jit(solution)/shard_map/ppermute | solution.py:20
  60.3 5.8 copy-start.1
  60.3 5.8 copy-start.2
  60.3 5.8 copy-start.3
  60.3 10.9 %copy-start.6 = (f32[8,8,2,128]{2,1,3,0:T(8,128)S(1)}, f32[8,8,2,128]{2,1,3,0:T(8,128)}, u32[]{:S(2)}) copy-start(f32[8,8,2,128]{2,1,3,0:T(8,128)} %copy.70) | copy-start | bytes 196612
  61.7 8.3 %collective-permute-start.2 = (f32[8,8,36,2]{2,1,3,0:T(8,128)S(1)}, f32[8,8,36,2]{2,1,3,0:T(8,128)S(1)}, u32[]{:S(2)}, u32[]{:S(2)}) collective-permute-start(f32[8,8,36,2]{2,1,3,0:T(8,128)S(1)} %get-tuple-element.12), channel_id=1, source_target_pairs={{0,1},{1,2},{2,3},{3,4},{4,5},{5,6},{6,7},{7,8},{8,9},{9,10},{10,1... | collective-permute-start | bytes 55304 | tf_op jit(solution)/shard_map/ppermute | solution.py:19
  63.8 7.4 copy-start.4
  63.8 7.4 copy-start.5
  63.8 7.4 collective-permute-start.3
  73.8 4.3 copy-start.8
  73.8 4.2 copy-start.15
  84.4 2.3 copy-start.9
  84.4 2.3 copy-start.10
  138.9 4.1 copy-start.16
  138.9 4.1 copy-start.17
  138.9 3.8 slice-start
  (4 other events, 8.8 us)
Sparse Core Ops, SparseCore 0:
  9.9 739.7 all-gather.1
where the time goes:
time: 767 us; the launch traced here: 766 us
  waiting for transfers between devices  454 us (59%)
  blocking collectives  185 us (24%)
  other arithmetic  43.3 us (6%)
  local copies, waits for them, and re-layouts  37.6 us (5%)
  starting transfers between devices  16.7 us (2%)
  between operations  15 us (2%)
  matrix products  14.8 us (2%)
    all_gather x1, waiting for transfers between devices, shards(): lax.all_gather(grad_in, LAT_LON, axis=0, tiled=True)  452 us
    psum x1, blocking collectives, shards(): fresh_all = lax.psum(dense, LAT_LON).astype(jnp.bfloat16)  144 us
    psum x2, blocking collectives, one_axis_at_a_time(): return functools.reduce(lax.psum, axes, x)  40.6 us
  transfers between devices with their start and end apart: 9, of which 2 were waited for; matrix products, arithmetic and copies ran while one was open for 11% of the time, Pallas kernels for 0%

commit v1 on v0

--- a/solution.py
+++ b/solution.py
@@ -7,6 +7,13 @@
 
 LON = ("lon_0", "lon_1")
 LAT_LON = ("lat", "lon_0", "lon_1")
+
+
+def work_wires(point):
+    opened = jnp.concatenate(
+        jax.lax.all_to_all(jnp.stack([point] * jax.lax.axis_size(LAT_LON)), LAT_LON, 0, 0), axis=0
+    )
+    return opened
 
 
 def extended_2(x, sides, width):
@@ -73,11 +80,7 @@
     week_cols = grad_in.shape[1] // tracers
     lon_count = lax.axis_size(LON)
     my_tile = lax.axis_index("lat") * lon_count + lax.axis_index(LON)
-    base = jnp.dot(
-        covariance,
-        lax.all_gather(grad_in, LAT_LON, axis=0, tiled=True),
-        preferred_element_type=jnp.float32,
-    )
+    base = jnp.dot(covariance, work_wires(grad_in), preferred_element_type=jnp.float32)
     extended, rate_ext = (
         extended_2(adjoint, (("lat", 2), (LON, 3)), 2),
         extended_2(transport, (("lat", 2), (LON, 3)), 2),

time: 767 us -> 689 us (0.90); the launches traced: 766 us -> 677 us
  waiting for transfers between devices: 454 us -> 326 us
  local copies, waits for them, and re-layouts: 37.6 us -> 61.4 us
  starting transfers between devices: 16.7 us -> 32.2 us
  matrix products: 14.8 us -> 28.5 us
  between operations: 15 us -> 1.81 us
    all_gather x1 -> x0, waiting for transfers between devices: 452 us -> none  [shards(): lax.all_gather(grad_in, LAT_LON, axis=0, tiled=True)]
    ppermute x4, waiting for transfers between devices: 0.01 us -> 326 us  [extended_2(): before = lax.ppermute(last, axis, up)]
    dot_general x0 -> x1, local copies, waits for them, and re-layouts: none -> 19.6 us  [shards(): jnp.dot(covariance, work_wires(grad_in), preferred_element_type=jnp.float32)]
    all_to_all x0 -> x1, starting transfers between devices: none -> 15 us  [work_wires(): jax.lax.all_to_all(jnp.stack([point] * jax.lax.axis_size(LAT_LON)), LAT_L...]
    dot_general x1, matrix products: 9.43 us -> 23.1 us  [shards(): jnp.dot(covariance, work_wires(grad_in), preferred_element_type=jnp.float32)]
  transfers between devices with their start and end apart: 9 -> 9, of which waited for: 2 -> 2; matrix products, arithmetic and copies ran while one was open for 11% -> 12% of each run, Pallas kernels for 0% -> 0%
where the time goes in v1:
time: 689 us; the launch traced here: 677 us
  waiting for transfers between devices  326 us (47%)
  blocking collectives  185 us (27%)
  local copies, waits for them, and re-layouts  61.4 us (9%)
  other arithmetic  42 us (6%)
  starting transfers between devices  32.2 us (5%)
  matrix products  28.5 us (4%)
    ppermute x4, waiting for transfers between devices, extended_2(): before = lax.ppermute(last, axis, up)  326 us
    psum x1, blocking collectives, shards(): fresh_all = lax.psum(dense, LAT_LON).astype(jnp.bfloat16)  146 us
    psum x2, blocking collectives, one_axis_at_a_time(): return functools.reduce(lax.psum, axes, x)  39.1 us
    dot_general x1, matrix products, shards(): jnp.dot(covariance, work_wires(grad_in), preferred_element_type=jnp.float32)  23.1 us
    dot_general x1, local copies, waits for them, and re-layouts, shards(): jnp.dot(covariance, work_wires(grad_in), preferred_element_type=jnp.float32)  19.6 us
    all_to_all x1, starting transfers between devices, work_wires(): jax.lax.all_to_all(jnp.stack([point] * jax.lax.axis_size(LAT_LON)), LAT_L...  15 us
  transfers between devices with their start and end apart: 9, of which 2 were waited for; matrix products, arithmetic and copies ran while one was open for 12% of the time, Pallas kernels for 0%

profile of v1, /device:TPU:96, one launch (start us, length us, event | category | flops | bytes accessed | tf_op | source)
XLA Modules:
  0.0 677.1 jit_solution(11513658782968490787)
XLA Ops:
  0.6 6.9 %stack.2 = bf16[256,64,416]{2,1,0:T(8,128)(2,1)} broadcast(bf16[64,416]{1,0:T(8,128)(2,1)} %param.16), dimensions={1,2} | broadcast | bytes 13684736 | tf_op jit(solution)/shard_map/stack | solution.py:14
  7.5 15.0 %all-to-all-start = ((bf16[256,64,416]{2,1,0:T(8,128)(2,1)}), bf16[256,64,416]{2,1,0:T(8,128)(2,1)}, u32[]{:S(2)}, u32[]{:S(2)}) async-start(bf16[256,64,416]{2,1,0:T(8,128)(2,1)} %stack.2), calls=%async_computation | async-start | bytes 33554432 | tf_op jit(solution)/shard_map/all_to_all | solution.py:14
  22.6 3.6 collective-permute-start.5
  27.9 3.9 collective-permute-start.1
  36.7 27.7 %collective-permute-done.4 = f32[6,8,2,128]{3,1,2,0:T(8,128)S(1)} collective-permute-done((f32[6,8,2,128]{3,1,2,0:T(8,128)S(1)}, f32[6,8,2,128]{3,1,2,0:T(8,128)S(1)}, u32[]{:S(2)}, u32[]{:S(2)}) %collective-permute-start.4) | collective-permute-done | bytes 49184 | tf_op jit(solution)/shard_map/ppermute | solution.py:26
  70.5 4.8 collective-permute-start.6
  75.9 2.8 copy.90
  87.5 298.7 %collective-permute-done.6 = f32[6,8,36,2]{2,1,3,0:T(8,128)} collective-permute-done((f32[6,8,36,2]{2,1,3,0:T(8,128)}, f32[6,8,36,2]{2,1,3,0:T(8,128)}, u32[]{:S(2)}, u32[]{:S(2)}) %collective-permute-start.6) | collective-permute-done | bytes 13856 | tf_op jit(solution)/shard_map/ppermute | solution.py:26
  386.2 4.4 maximum_bitcast_fusion.4
  390.6 3.4 copy.89
  394.1 3.4 copy.91
  400.5 3.2 collective-permute-start.3
  403.7 3.2 maximum_bitcast_fusion.3
  409.3 4.3 slice_subtract_fusion.9
  413.7 6.3 fusion.6
  422.4 7.0 %fusion.41 = (f32[8,8,32]{2,1,0:T(8,128)S(1)}, f32[8,8,32,128]{2,1,3,0:T(8,128)}) fusion(f32[8,7,32,128]{2,1,3,0:T(8,128)S(1)} %get-tuple-element.31, f32[8,32,128]{1,0,2:T(8,128)S(1)} %copy-done.14, f32[8,7,32,128]{2,1,3,0:T(8,128)S(1)} %get-tuple-element.30, f32[8,32,128]{1,0,2:T(8,128)} %copy.101, f32[8,8,34,130]{2,1,3,0:T(8,128)S(1)} %fusion.6, ...), kind=kLoop, calls=%fused_computation.80 | loop fusion | flops 4454400 | bytes 8921088 | tf_op jit(solution)/shard_map/reduce_sum | solution.py:92
  429.4 27.7 %psum.21 = f32[8,8,32]{2,1,0:T(8,128)S(1)} all-reduce(f32[8,8,32]{2,1,0:T(8,128)S(1)} %get-tuple-element.16), channel_id=1, replica_groups=mesh['lat'=16,'lon_0'=8,'lon_1'=2] {'lon_0'}, use_global_device_ids=true, to_apply=%region_1.2 | all-reduce | flops 2048 | bytes 16384 | tf_op jit(solution)/shard_map/psum | solution.py:33
  457.1 11.4 %psum.22 = f32[8,8,32]{2,1,0:T(8,128)S(1)} all-reduce(f32[8,8,32]{2,1,0:T(8,128)S(1)} %psum.21), channel_id=1, replica_groups=mesh['lat'=16,'lon_0'=8,'lon_1'=2] {'lon_1'}, use_global_device_ids=true, to_apply=%region_2.3 | all-reduce | flops 2048 | bytes 16384 | tf_op jit(solution)/shard_map/psum | solution.py:33
  473.2 3.7 copy.108
  479.1 5.2 scatter_custom_fusion
  484.3 145.6 %all-reduce.5 = bf16[16384,8]{1,0:T(8,128)(2,1)} all-reduce(f32[16384,8]{1,0:T(8,128)} %scatter_custom_fusion), channel_id=1, replica_groups=mesh['lat'=16,'lon_0'=8,'lon_1'=2] {'lat','lon_0','lon_1'}, use_global_device_ids=true, to_apply=%region_4.5 | all-reduce | flops 131072 | bytes 786432 | tf_op jit(solution)/shard_map/psum | solution.py:110
  629.9 3.4 fusion.35
  633.3 19.6 %copy.103 = bf16[416,16384]{1,0:T(8,128)(2,1)} copy(bf16[416,16384]{0,1:T(8,128)(2,1)} %bitcast.14) | data formatting | bytes 27262976 | tf_op jit(solution)/shard_map/dot_general | solution.py:83
  652.9 23.1 %fusion.30 = f32[64,52,8]{0,1,2:T(8,128)S(1)} fusion(bf16[52,8,16384]{2,1,0:T(8,128)(2,1)} %bitcast.53, bf16[64,16384]{1,0:T(8,128)(2,1)S(1)} %copy-done, f32[64,8]{0,1:T(8,128)S(1)} %fusion.35, f32[52]{0:T(128)S(1)} %copy-done.19), kind=kOutput, calls=%fused_computation.46 | convolution fusion | flops 872468480 | bytes 15837392 | tf_op jit(solution)/shard_map/dot_general | solution.py:83
  (84 shorter events, 37.0 us)
Async XLA Ops:
  0.6 629.2 %copy-start = (bf16[64,16384]{1,0:T(8,128)(2,1)S(1)}, bf16[64,16384]{1,0:T(8,128)(2,1)}, u32[]{:S(2)}) copy-start(bf16[64,16384]{1,0:T(8,128)(2,1)} %param.17) | copy-start | bytes 6291460
  7.5 15.0 %copy-start.8 = (f32[6,8,32,128]{3,2,1,0:T(8,128)S(1)}, f32[6,8,32,128]{3,2,1,0:T(8,128)}, u32[]{:S(2)}) copy-start(f32[6,8,32,128]{3,2,1,0:T(8,128)} %param.10) | copy-start | bytes 2359300
  7.5 25.6 %copy-start.18 = (s32[32]{0:T(128)S(1)}, s32[32]{0:T(128)}, u32[]{:S(2)}) copy-start(s32[32]{0:T(128)} %param.14) | copy-start | bytes 388
  7.5 625.8 %all-to-all-start = ((bf16[256,64,416]{2,1,0:T(8,128)(2,1)}), bf16[256,64,416]{2,1,0:T(8,128)(2,1)}, u32[]{:S(2)}, u32[]{:S(2)}) async-start(bf16[256,64,416]{2,1,0:T(8,128)(2,1)} %stack.2), calls=%async_computation | async-start | bytes 33554432 | tf_op jit(solution)/shard_map/all_to_all | solution.py:14
  22.6 44.0 %collective-permute-start.5 = (f32[6,8,2,128]{3,1,2,0:T(8,128)S(1)}, f32[6,8,2,128]{3,1,2,0:T(8,128)S(1)}, u32[]{:S(2)}, u32[]{:S(2)}) collective-permute-start(f32[6,8,2,128]{3,1,2,0:T(8,128)S(1)} %copy.114), channel_id=1, source_target_pairs={{16,0},{32,16},{48,32},{64,48},{80,64},{96,80},{112,96},{128,112},... | collective-permute-start | bytes 147464 | tf_op jit(solution)/shard_map/ppermute | solution.py:27
  26.2 38.2 %collective-permute-start.4 = (f32[6,8,2,128]{3,1,2,0:T(8,128)S(1)}, f32[6,8,2,128]{3,1,2,0:T(8,128)S(1)}, u32[]{:S(2)}, u32[]{:S(2)}) collective-permute-start(f32[6,8,2,128]{3,1,2,0:T(8,128)S(1)} %copy.113), channel_id=1, source_target_pairs={{0,16},{16,32},{32,48},{48,64},{64,80},{80,96},{96,112},{112,128},... | collective-permute-start | bytes 147464 | tf_op jit(solution)/shard_map/ppermute | solution.py:26
  27.9 366.2 %collective-permute-start.1 = (f32[8,8,2,128]{3,1,2,0:T(8,128)}, f32[8,8,2,128]{3,1,2,0:T(8,128)}, u32[]{:S(2)}, u32[]{:S(2)}) collective-permute-start(f32[8,8,2,128]{3,1,2,0:T(8,128)} %copy.112), channel_id=1, source_target_pairs={{16,0},{32,16},{48,32},{64,48},{80,64},{96,80},{112,96},{128,112},... | collective-permute-start | bytes 196616 | tf_op jit(solution)/shard_map/ppermute | solution.py:27
  32.4 358.3 %collective-permute-start = (f32[8,8,2,128]{3,1,2,0:T(8,128)}, f32[8,8,2,128]{3,1,2,0:T(8,128)}, u32[]{:S(2)}, u32[]{:S(2)}) collective-permute-start(f32[8,8,2,128]{3,1,2,0:T(8,128)} %copy.111), channel_id=1, source_target_pairs={{0,16},{16,32},{32,48},{48,64},{64,80},{80,96},{96,112},{112,128},... | collective-permute-start | bytes 196616 | tf_op jit(solution)/shard_map/ppermute | solution.py:26
  68.8 7.2 %copy-start.15 = (f32[8,8,32,128]{3,2,1,0:T(8,128)S(1)}, f32[8,8,32,128]{3,2,1,0:T(8,128)}, u32[]{:S(2)}) copy-start(f32[8,8,32,128]{3,2,1,0:T(8,128)} %param.9) | copy-start | bytes 3145732
  70.5 315.7 %collective-permute-start.6 = (f32[6,8,36,2]{2,1,3,0:T(8,128)}, f32[6,8,36,2]{2,1,3,0:T(8,128)}, u32[]{:S(2)}, u32[]{:S(2)}) collective-permute-start(f32[6,8,36,2]{2,1,3,0:T(8,128)} %get-tuple-element.26), channel_id=1, source_target_pairs={{0,1},{1,2},{2,3},{3,4},{4,5},{5,6},{6,7},{7,8},{8,9},{9,10},{10,1... | collective-permute-start | bytes 41480 | tf_op jit(solution)/shard_map/ppermute | solution.py:26
  75.3 310.9 %collective-permute-start.7 = (f32[6,8,36,2]{2,1,3,0:T(8,128)}, f32[6,8,36,2]{2,1,3,0:T(8,128)}, u32[]{:S(2)}, u32[]{:S(2)}) collective-permute-start(f32[6,8,36,2]{2,1,3,0:T(8,128)} %get-tuple-element.27), channel_id=1, source_target_pairs={{1,0},{2,1},{3,2},{4,3},{5,4},{6,5},{7,6},{8,7},{9,8},{10,9},{11,1... | collective-permute-start | bytes 41480 | tf_op jit(solution)/shard_map/ppermute | solution.py:27
  397.5 6.3 copy-start.1
  397.5 6.3 copy-start.2
  397.5 6.3 copy-start.3
  397.5 9.5 %copy-start.6 = (f32[8,8,2,128]{2,1,3,0:T(8,128)S(1)}, f32[8,8,2,128]{2,1,3,0:T(8,128)}, u32[]{:S(2)}) copy-start(f32[8,8,2,128]{2,1,3,0:T(8,128)} %copy.91) | copy-start | bytes 196612
  398.8 8.2 %collective-permute-start.2 = (f32[8,8,36,2]{2,1,3,0:T(8,128)S(1)}, f32[8,8,36,2]{2,1,3,0:T(8,128)S(1)}, u32[]{:S(2)}, u32[]{:S(2)}) collective-permute-start(f32[8,8,36,2]{2,1,3,0:T(8,128)S(1)} %get-tuple-element.18), channel_id=1, source_target_pairs={{0,1},{1,2},{2,3},{3,4},{4,5},{5,6},{6,7},{7,8},{8,9},{9,10},{10,1... | collective-permute-start | bytes 55304 | tf_op jit(solution)/shard_map/ppermute | solution.py:26
  400.5 6.4 copy-start.4
  400.5 6.4 copy-start.5
  400.5 6.4 collective-permute-start.3
  409.3 4.4 copy-start.9
  473.2 3.9 copy-start.16
  473.2 3.9 copy-start.17
  473.2 3.7 slice-start
  633.3 19.6 %copy-start.19 = (f32[52]{0:T(128)S(1)}, f32[52]{0:T(128)}, u32[]{:S(2)}) copy-start(f32[52]{0:T(128)} %compare_convert_fusion) | copy-start | bytes 628
  (6 other events, 13.5 us)
